TPU v7x, 32 devices: a whole 2x2x4 slice. The times are simulated.
32 devices in a mesh: mu: 8 (over y, x, core), nu: 4 (over z).
Axes of the slice: x: 2, y: 2, z: 4, core: 2. Of those that a mesh axis runs over, the one named last changes fastest.
Arguments:
- earlier_vectors: float32 [1024, 1024, 512], P('mu', 'nu'), may hold values from -0.72 to 0.72
- pivot_integral_columns: float32 [1024, 1024, 256], P('mu', 'nu'), may hold values from -6 to 6
- diagonal: float32 [1024, 1024], P('mu', 'nu'), may hold values from 2 to 60
- orbitals: float32 [1024, 40], replicated, may hold values from -0.1875 to 0.1875
- pivots: int32 [256], replicated, may hold values from 0 to 1048575, as said below
Outputs:
- transformed: float32 [256, 820], P(('mu', 'nu'))
- updated_diagonal: float32 [1024, 1024], P('mu', 'nu')
Inputs may be any that keep to these rules, and one draw needn't show every extreme that they name: The pivots are distinct. The pairs held by one device (a block of 128 first by 256 second AO indices) contain at most 32 pivots, and some block contains exactly 32.
All inputs are finite; a program needn't handle non-finite values.
Results may differ from a plain program's by a relative error of at most 0.0001.
Values sent between devices are 32-bit elements; how exact they have to be, the bound alone decides.
A program may use at most 256 MiB of HBM per device.

v0:
```python
import jax
import jax.numpy as jnp
import numpy as np
from jax import lax
from jax.sharding import PartitionSpec as P

precise = lax.Precision.HIGHEST


def local(earlier_vectors, pivot_integral_columns, diagonal, orbitals, pivots):
    orbital_rows_mu, cols_nu, preceding = earlier_vectors.shape
    pivot_count = pivots.shape[0]
    ao_count, active = orbitals.shape
    size_mu = lax.axis_size("mu")
    size_nu = lax.axis_size("nu")
    index_mu = lax.axis_index("mu")
    index_nu = lax.axis_index("nu")
    pivot_mu = pivots // ao_count
    pivot_nu = pivots % ao_count
    owner_mu = pivot_mu // orbital_rows_mu
    owner_nu = pivot_nu // cols_nu
    local_row = pivot_mu % orbital_rows_mu * cols_nu + pivot_nu % cols_nu
    is_owned = (owner_mu == index_mu) & (owner_nu == index_nu)
    flat_vectors = earlier_vectors.reshape(orbital_rows_mu * cols_nu, preceding)
    flat_diag = diagonal.reshape(orbital_rows_mu * cols_nu)
    picked = jnp.take(flat_vectors, local_row, axis=0)
    picked_diag = jnp.take(flat_diag, local_row)
    masked = jnp.where(is_owned[:, None], picked, 0.0)
    masked_diag = jnp.where(is_owned, picked_diag, 0.0)
    pivot_rows, pivot_diag = lax.psum((masked, masked_diag), ("mu", "nu"))
    residual_diag = pivot_diag - jnp.sum(pivot_rows * pivot_rows, axis=1)
    scaling = lax.rsqrt(jnp.maximum(residual_diag, 1.0))
    update = lax.dot_general(flat_vectors, pivot_rows, (((1,), (1,)), ((), ())), precision=precise)
    flat_columns = pivot_integral_columns.reshape(orbital_rows_mu * cols_nu, pivot_count)
    fresh_vectors = (flat_columns - update) * scaling[None, :]
    updated_diagonal = (flat_diag - jnp.sum(fresh_vectors * fresh_vectors, axis=1)).reshape(
        orbital_rows_mu, cols_nu
    )
    basis_left_index = lax.dynamic_slice_in_dim(
        orbitals, index_mu * orbital_rows_mu, orbital_rows_mu, 0
    )
    orbit_nu = lax.dynamic_slice_in_dim(orbitals, index_nu * cols_nu, cols_nu, 0)
    fresh_blocks = fresh_vectors.reshape(orbital_rows_mu, cols_nu, pivot_count)
    half_done = jnp.einsum("mp,mnj->jpn", basis_left_index, fresh_blocks, precision=precise)
    row_index, col_index = np.tril_indices(active)
    full_done = jnp.einsum("nq,jpn->jpq", orbit_nu, half_done, precision=precise)
    pair_values = full_done[:, row_index, col_index]
    pair_count = row_index.shape[0]
    per_device = pivot_count // (size_mu * size_nu)
    split_mu = pair_values.reshape(size_mu, size_nu * per_device, pair_count)
    summed = lax.psum_scatter(split_mu, "mu", scatter_dimension=0, tiled=True)
    split_nu = summed.reshape(size_nu, per_device, pair_count)
    transformed = lax.psum_scatter(split_nu, "nu", scatter_dimension=0, tiled=True).reshape(
        per_device, pair_count
    )
    return (transformed, updated_diagonal)


def solution(mesh):
    placed = (P("mu", "nu", None), P("mu", "nu", None), P("mu", "nu"), P(), P())
    return jax.shard_map(
        local,
        mesh=mesh,
        in_specs=placed,
        out_specs=(P(("mu", "nu"), None), P("mu", "nu")),
        check_vma=False,
    )
```

profile of v0, /device:TPU:0, one launch (start us, length us, event | category | flops | bytes accessed | tf_op | source)
XLA Modules:
  0.0 358.0 jit_solution(5363346834168782279)
XLA Ops:
  7.2 0.0 copy-start
  7.2 0.0 all-reduce.3.cloned.1.call-start
  7.2 0.7 compare_select_fusion
  8.0 1.0 copy.21
  9.0 1.7 gather_fusion.1
  10.7 2.8 gather_fusion
  13.5 0.7 select_select_fusion.1
  14.2 0.9 select_select_fusion
  15.1 0.0 all-reduce.3.cloned.1.call-update
  15.1 0.0 reduce-scatter.5.cloned.1.call-start
  15.2 31.1 %copy.20 = f32[32768,256]{0,1:T(8,128)} copy(f32[32768,256]{1,0:T(8,128)} %bitcast.33) | data formatting | bytes 67108864 | tf_op jit(solution)/shard_map/reshape | solution.py:34
  46.2 42.1 %psum.15 = f32[256]{0:T(256)S(1)} all-reduce(f32[256]{0:T(256)S(1)} %get-tuple-element.2), channel_id=1, replica_groups=mesh['mu'=8,'nu'=4] {'mu','nu'}, use_global_device_ids=true, to_apply=%region_1.2 | all-reduce | flops 256 | bytes 2048 | tf_op jit(solution)/shard_map/psum | solution.py:30
  88.3 58.7 %all-reduce.3.cloned.1.call-done = f32[256,512]{1,0:T(8,128)} async-done(((f32[256,512]{1,0:T(8,128)}), f32[256,512]{1,0:T(8,128)}) %all-reduce.3.cloned.1.call-update) | async-done | bytes 524304 | tf_op jit(solution)/shard_map/psum | solution.py:30
  147.1 1.2 multiply_reduce_fusion.1
  148.2 65.5 %multiply_reduce_fusion = (f32[32768]{0:T(1024)S(1)}, f32[32768,256]{0,1:T(8,128)}) fusion(f32[256]{0:T(256)S(1)} %maximum_rsqrt_fusion, f32[32768,256]{0,1:T(8,128)} %copy.20, f32[256,512]{1,0:T(8,128)} %all-reduce.3.cloned.1.call-done, f32[32768,512]{1,0:T(8,128)} %bitcast.1), kind=kOutput, calls=%fused_computation.6 | convolution fusion | flops 51573129216 | bytes 134874112 | tf_op jit(solution)/shard_map/dot_general | solution.py:33
  213.8 30.5 %copy.22 = f32[32,8,128,256]{3,2,1,0:T(8,128)} copy(f32[32,8,128,256]{3,1,2,0:T(8,128)} %bitcast.32) | data formatting | bytes 67108864
  244.3 0.0 copy-done
  244.3 0.0 copy-start.1
  244.3 0.0 copy-start.2
  244.3 23.0 %fusion.6 = f32[256,256,40]{0,2,1:T(8,128)S(1)} fusion(f32[128,256,256]{1,0,2:T(8,128)} %bitcast.31, f32[1024,40]{0,1:T(8,128)S(1)} %copy-done, s32[]{:T(128)S(6)} %select_n.71), kind=kOutput, calls=%fused_computation.13 | convolution fusion | flops 4026531840 | bytes 44060676 | tf_op jit(solution)/shard_map/mp,mnj->jpn/dot_general | solution.py:44
  267.3 10.0 %fusion.2 = f32[256,40,40]{2,1,0:T(8,128)} fusion(f32[256,256,40]{0,2,1:T(8,128)S(1)} %fusion.6, f32[1024,40]{0,1:T(8,128)S(1)} %copy-done, s32[]{:T(128)S(6)} %select_n.72), kind=kOutput, calls=%fused_computation.7 | convolution fusion | flops 1258291200 | bytes 12165124 | tf_op jit(solution)/shard_map/nq,jpn->jpq/dot_general | solution.py:46
  277.3 5.0 %copy.19 = f32[256,40,40]{0,2,1:T(8,128)S(1)} copy(f32[256,40,40]{2,1,0:T(8,128)} %fusion.2) | data formatting | bytes 3276800 | tf_op jit(solution)/shard_map/nq,jpn->jpq/dot_general | solution.py:46
  282.3 0.0 copy-done.1
  282.3 11.0 %gather_fusion.2 = f32[820,256]{1,0:T(8,128)S(1)} fusion(f32[256,40,40]{0,2,1:T(8,128)S(1)} %copy.19, s32[820]{0:T(1024)S(1)} %copy-done.1), kind=kCustom, calls=%fused_computation.2 | custom fusion | bytes 1685920 | tf_op jit(solution)/shard_map/gather | solution.py:47
  293.3 1.2 copy.17
  294.5 0.0 reduce-scatter.5.cloned.1.call-update
  294.6 0.0 reduce-scatter.7.cloned.1.call-start
  294.6 34.6 %reduce-scatter.5.cloned.1.call-done = f32[1,32,820]{2,1,0:T(8,128)} async-done(((f32[8,32,820]{2,1,0:T(8,128)}), f32[1,32,820]{2,1,0:T(8,128)}) %reduce-scatter.5.cloned.1.call-update) | async-done | bytes 104976 | tf_op jit(solution)/shard_map/reduce_scatter | solution.py:51
  329.2 0.0 reduce-scatter.7.cloned.1.call-update
  329.2 0.0 copy-done.2
  329.3 0.7 sub.29
  329.9 21.5 %reduce-scatter.7.cloned.1.call-done = f32[1,8,820]{2,1,0:T(8,128)} async-done(((f32[4,8,820]{2,1,0:T(8,128)}), f32[1,8,820]{2,1,0:T(8,128)}) %reduce-scatter.7.cloned.1.call-update) | async-done | bytes 26256
  (3 shorter events, 0.1 us)
Async XLA Ops:
  7.2 237.1 %copy-start = (f32[1024,40]{0,1:T(8,128)S(1)}, f32[1024,40]{0,1:T(8,128)}, u32[]{:S(2)}) copy-start(f32[1024,40]{0,1:T(8,128)} %param.12) | copy-start | bytes 491524
  7.2 139.9 %all-reduce.3.cloned.1.call-start = ((), (), s32[]{:S(2)}) async-start(), calls=%async_computation.2 | async-start | bytes 1048576 | tf_op jit(solution)/shard_map/psum | solution.py:30
  15.1 314.1 %reduce-scatter.5.cloned.1.call-start = ((), (), s32[]{:S(2)}) async-start(), calls=%async_computation.3 | async-start | bytes 1032192 | tf_op jit(solution)/shard_map/reduce_scatter | solution.py:51
  244.3 38.0 %copy-start.1 = (s32[820]{0:T(1024)S(1)}, s32[820]{0:T(1024)}, u32[]{:S(2)}) copy-start(s32[820]{0:T(1024)} %constant.144) | copy-start | bytes 9844
  244.3 85.0 %copy-start.2 = (f32[128,256]{1,0:T(8,128)S(1)}, f32[128,256]{1,0:T(8,128)}, u32[]{:S(2)}) copy-start(f32[128,256]{1,0:T(8,128)} %param.11) | copy-start | bytes 393220
  294.6 56.9 %reduce-scatter.7.cloned.1.call-start = ((), (), s32[]{:S(2)}) async-start(), calls=%async_computation.4 | async-start | bytes 143360
Sparse Core Ops, SparseCore 0:
  15.2 131.7 all-reduce.2
  294.7 34.4 reduce-scatter.4
  332.0 19.4 reduce-scatter.6
where the time goes:
time: 359 us; the launch traced here: 358 us
  waiting for transfers between devices  115 us (32%)
  matrix products  98.5 us (27%)
  local copies, waits for them, and re-layouts  84.3 us (23%)
  blocking collectives  42.1 us (12%)
  between operations  13.8 us (4%)
  other arithmetic  4.23 us (1%)
    dot_general x1, matrix products, local(): lax.dot_general(flat_vectors, pivot_rows, (((1,), (1,)), ((), ())), preci...  65.5 us
    psum x1, waiting for transfers between devices, local(): pivot_rows, pivot_diag = lax.psum((masked, masked_diag), ('mu', 'nu'))  58.7 us
    psum x1, blocking collectives, local(): pivot_rows, pivot_diag = lax.psum((masked, masked_diag), ('mu', 'nu'))  42.1 us
    reduce_scatter x1, waiting for transfers between devices, local(): summed = lax.psum_scatter(split_mu, 'mu', scatter_dimension=0, tiled=True)  34.6 us
    unnamed x8, local copies, waits for them, and re-layouts  31.5 us
    reshape x1, local copies, waits for them, and re-layouts, local(): pivot_integral_columns.reshape(orbital_rows_mu * cols_nu, pivot_count)  31.1 us
    dot_general x1, matrix products, local(): jnp.einsum('mp,mnj->jpn', basis_left_index, fresh_blocks, precision=precise)  23 us
    unnamed x4, waiting for transfers between devices  21.6 us
  transfers between devices with their start and end apart: 3, of which 3 were waited for; matrix products, arithmetic and copies ran while one was open for 9% of the time, Pallas kernels for 0%

commit v1 on v0

--- a/solution.py
+++ b/solution.py
@@ -27,7 +27,7 @@
     picked_diag = jnp.take(flat_diag, local_row)
     masked = jnp.where(is_owned[:, None], picked, 0.0)
     masked_diag = jnp.where(is_owned, picked_diag, 0.0)
-    pivot_rows, pivot_diag = lax.psum((masked, masked_diag), ("mu", "nu"))
+    pivot_rows, pivot_diag = lax.psum(lax.psum((masked, masked_diag), "nu"), "mu")
     residual_diag = pivot_diag - jnp.sum(pivot_rows * pivot_rows, axis=1)
     scaling = lax.rsqrt(jnp.maximum(residual_diag, 1.0))
     update = lax.dot_general(flat_vectors, pivot_rows, (((1,), (1,)), ((), ())), precision=precise)

time: 359 us -> 326 us (0.908)
  blocking collectives: 42.1 us -> 22.6 us
  waiting for transfers between devices: 115 us -> 102 us
    psum x1 -> x2, blocking collectives: 42.1 us -> 22.6 us  [the longest x1 12.1 us: local(): lax.psum(lax.psum((masked, masked_diag), 'nu'), 'mu')]
    psum x1 -> x2, waiting for transfers between devices: 58.7 us -> 45.3 us  [the longest x1 41.3 us: local(): lax.psum((masked, masked_diag), 'nu')]
    unnamed x4 -> x5, waiting for transfers between devices: 21.6 us -> 21.4 us
  transfers between devices with their start and end apart: 3 -> 4, of which waited for: 3 -> 4; matrix products, arithmetic and copies ran while one was open for 9% -> 10% of each run, Pallas kernels for 0% -> 0%
where the time goes in v1:
time: 326 us; the launch traced here: 325 us
  waiting for transfers between devices  102 us (31%)
  matrix products  98.5 us (30%)
  local copies, waits for them, and re-layouts  84.3 us (26%)
  blocking collectives  22.6 us (7%)
  between operations  13.9 us (4%)
  other arithmetic  4.21 us (1%)
    dot_general x1, matrix products, local(): lax.dot_general(flat_vectors, pivot_rows, (((1,), (1,)), ((), ())), preci...  65.5 us
    psum x1, waiting for transfers between devices, local(): lax.psum((masked, masked_diag), 'nu')  41.3 us
    reduce_scatter x1, waiting for transfers between devices, local(): summed = lax.psum_scatter(split_mu, 'mu', scatter_dimension=0, tiled=True)  34.9 us
    unnamed x8, local copies, waits for them, and re-layouts  31.5 us
    reshape x1, local copies, waits for them, and re-layouts, local(): pivot_integral_columns.reshape(orbital_rows_mu * cols_nu, pivot_count)  31.1 us
    dot_general x1, matrix products, local(): jnp.einsum('mp,mnj->jpn', basis_left_index, fresh_blocks, precision=precise)  23 us
    unnamed x5, waiting for transfers between devices  21.4 us
    gather x2, local copies, waits for them, and re-layouts, local(): pair_values = full_done[:, row_index, col_index]  12.2 us
  transfers between devices with their start and end apart: 4, of which 4 were waited for; matrix products, arithmetic and copies ran while one was open for 10% of the time, Pallas kernels for 0%

profile of v1, /device:TPU:0, one launch (start us, length us, event | category | flops | bytes accessed | tf_op | source)
XLA Modules:
  0.0 325.3 jit_solution(8566774259307808949)
XLA Ops:
  7.2 0.0 copy-start
  7.2 0.0 all-reduce.4.cloned.1.call-start
  7.2 0.7 compare_select_fusion
  8.0 1.0 copy.21
  9.0 1.7 gather_fusion.1
  10.7 2.8 gather_fusion
  13.5 0.7 select_select_fusion.1
  14.2 0.9 select_select_fusion
  15.1 0.0 all-reduce.4.cloned.1.call-update
  15.1 0.0 all-reduce.6.cloned.1.call-start
  15.2 41.3 %all-reduce.4.cloned.1.call-done = f32[256,512]{1,0:T(8,128)} async-done(((f32[256,512]{1,0:T(8,128)}), f32[256,512]{1,0:T(8,128)}) %all-reduce.4.cloned.1.call-update) | async-done | bytes 524304 | tf_op jit(solution)/shard_map/psum | solution.py:30
  56.5 0.0 all-reduce.6.cloned.1.call-update
  56.5 0.0 reduce-scatter.5.cloned.1.call-start
  56.6 31.1 %copy.20 = f32[32768,256]{0,1:T(8,128)} copy(f32[32768,256]{1,0:T(8,128)} %bitcast.33) | data formatting | bytes 67108864 | tf_op jit(solution)/shard_map/reshape | solution.py:34
  87.6 10.6 %psum.30 = f32[256]{0:T(256)S(1)} all-reduce(f32[256]{0:T(256)S(1)} %get-tuple-element.2), channel_id=1, replica_groups=mesh['mu'=8,'nu'=4] {'nu'}, use_global_device_ids=true, to_apply=%region_2.3 | all-reduce | flops 256 | bytes 2048 | tf_op jit(solution)/shard_map/psum | solution.py:30
  98.2 12.1 %psum.31 = f32[256]{0:T(256)S(1)} all-reduce(f32[256]{0:T(256)S(1)} %psum.30), channel_id=1, replica_groups=mesh['mu'=8,'nu'=4] {'mu'}, use_global_device_ids=true, to_apply=%region_3.4 | all-reduce | flops 256 | bytes 2048 | tf_op jit(solution)/shard_map/psum | solution.py:30
  110.3 4.0 %all-reduce.6.cloned.1.call-done = f32[256,512]{1,0:T(8,128)} async-done(((f32[256,512]{1,0:T(8,128)}), f32[256,512]{1,0:T(8,128)}) %all-reduce.6.cloned.1.call-update) | async-done | bytes 524304 | tf_op jit(solution)/shard_map/psum | solution.py:30
  114.2 1.2 multiply_reduce_fusion.1
  115.4 65.5 %multiply_reduce_fusion = (f32[32768]{0:T(1024)S(1)}, f32[32768,256]{0,1:T(8,128)}) fusion(f32[256]{0:T(256)S(1)} %maximum_rsqrt_fusion, f32[32768,256]{0,1:T(8,128)} %copy.20, f32[256,512]{1,0:T(8,128)} %all-reduce.6.cloned.1.call-done, f32[32768,512]{1,0:T(8,128)} %bitcast.1), kind=kOutput, calls=%fused_computation.6 | convolution fusion | flops 51573129216 | bytes 134874112 | tf_op jit(solution)/shard_map/dot_general | solution.py:33
  180.9 30.5 %copy.22 = f32[32,8,128,256]{3,2,1,0:T(8,128)} copy(f32[32,8,128,256]{3,1,2,0:T(8,128)} %bitcast.32) | data formatting | bytes 67108864
  211.4 0.0 copy-done
  211.4 0.0 copy-start.1
  211.4 0.0 copy-start.2
  211.5 23.0 %fusion.6 = f32[256,256,40]{0,2,1:T(8,128)S(1)} fusion(f32[128,256,256]{1,0,2:T(8,128)} %bitcast.31, f32[1024,40]{0,1:T(8,128)S(1)} %copy-done, s32[]{:T(128)S(6)} %select_n.71), kind=kOutput, calls=%fused_computation.13 | convolution fusion | flops 4026531840 | bytes 44060676 | tf_op jit(solution)/shard_map/mp,mnj->jpn/dot_general | solution.py:44
  234.4 10.0 %fusion.2 = f32[256,40,40]{2,1,0:T(8,128)} fusion(f32[256,256,40]{0,2,1:T(8,128)S(1)} %fusion.6, f32[1024,40]{0,1:T(8,128)S(1)} %copy-done, s32[]{:T(128)S(6)} %select_n.72), kind=kOutput, calls=%fused_computation.7 | convolution fusion | flops 1258291200 | bytes 12165124 | tf_op jit(solution)/shard_map/nq,jpn->jpq/dot_general | solution.py:46
  244.4 5.0 %copy.19 = f32[256,40,40]{0,2,1:T(8,128)S(1)} copy(f32[256,40,40]{2,1,0:T(8,128)} %fusion.2) | data formatting | bytes 3276800 | tf_op jit(solution)/shard_map/nq,jpn->jpq/dot_general | solution.py:46
  249.4 0.0 copy-done.1
  249.5 11.0 %gather_fusion.2 = f32[820,256]{1,0:T(8,128)S(1)} fusion(f32[256,40,40]{0,2,1:T(8,128)S(1)} %copy.19, s32[820]{0:T(1024)S(1)} %copy-done.1), kind=kCustom, calls=%fused_computation.2 | custom fusion | bytes 1685920 | tf_op jit(solution)/shard_map/gather | solution.py:47
  260.5 1.2 copy.17
  261.7 0.0 reduce-scatter.5.cloned.1.call-update
  261.7 0.0 reduce-scatter.7.cloned.1.call-start
  261.8 34.9 %reduce-scatter.5.cloned.1.call-done = f32[1,32,820]{2,1,0:T(8,128)} async-done(((f32[8,32,820]{2,1,0:T(8,128)}), f32[1,32,820]{2,1,0:T(8,128)}) %reduce-scatter.5.cloned.1.call-update) | async-done | bytes 104976 | tf_op jit(solution)/shard_map/reduce_scatter | solution.py:51
  296.7 0.0 reduce-scatter.7.cloned.1.call-update
  296.7 0.0 copy-done.2
  296.7 0.7 sub.29
  297.4 21.4 %reduce-scatter.7.cloned.1.call-done = f32[1,8,820]{2,1,0:T(8,128)} async-done(((f32[4,8,820]{2,1,0:T(8,128)}), f32[1,8,820]{2,1,0:T(8,128)}) %reduce-scatter.7.cloned.1.call-update) | async-done | bytes 26256
  (3 shorter events, 0.1 us)
Async XLA Ops:
  7.2 204.3 %copy-start = (f32[1024,40]{0,1:T(8,128)S(1)}, f32[1024,40]{0,1:T(8,128)}, u32[]{:S(2)}) copy-start(f32[1024,40]{0,1:T(8,128)} %param.12) | copy-start | bytes 491524
  7.2 49.3 %all-reduce.4.cloned.1.call-start = ((), (), s32[]{:S(2)}) async-start(), calls=%async_computation.2 | async-start | bytes 1048576 | tf_op jit(solution)/shard_map/psum | solution.py:30
  15.1 99.1 %all-reduce.6.cloned.1.call-start = ((), (), s32[]{:S(2)}) async-start(), calls=%async_computation.3 | async-start | bytes 1048576 | tf_op jit(solution)/shard_map/psum | solution.py:30
  56.5 240.1 %reduce-scatter.5.cloned.1.call-start = ((), (), s32[]{:S(2)}) async-start(), calls=%async_computation.4 | async-start | bytes 1032192 | tf_op jit(solution)/shard_map/reduce_scatter | solution.py:51
  211.4 38.0 %copy-start.1 = (s32[820]{0:T(1024)S(1)}, s32[820]{0:T(1024)}, u32[]{:S(2)}) copy-start(s32[820]{0:T(1024)} %constant.144) | copy-start | bytes 9844
  211.4 85.3 %copy-start.2 = (f32[128,256]{1,0:T(8,128)S(1)}, f32[128,256]{1,0:T(8,128)}, u32[]{:S(2)}) copy-start(f32[128,256]{1,0:T(8,128)} %param.11) | copy-start | bytes 393220
  261.7 57.0 %reduce-scatter.7.cloned.1.call-start = ((), (), s32[]{:S(2)}) async-start(), calls=%async_computation.5 | async-start | bytes 143360
Sparse Core Ops, SparseCore 0:
  15.2 41.2 all-reduce.3
  59.6 54.5 all-reduce.5
  261.9 34.7 reduce-scatter.4
  299.3 19.4 reduce-scatter.6
